TPU v7x, 256 devices: a whole 4x4x8 slice. The times are simulated.
256 devices in a mesh: batch: 32 (over z_lo, x, core), seq: 8 (over y, z_hi).
Axes of the slice: x: 4, y: 4, z: 8 (z_hi: 2, z_lo: 4; z = z_hi * 4 + z_lo), core: 2. Of those that a mesh axis runs over, the one named last changes fastest.
Arguments:
- tokens: bfloat16 [32, 4096, 2560], P('batch', 'seq'), may hold values from -6 to 6
- attn_in: bfloat16 [32, 4096, 2560], P('batch', 'seq'), may hold values from -6 to 6
- lengths: int32 [32], P('batch'), may hold values from 1024 to 4096
- norm_gain: float32 [2560], replicated, may hold values from 0.5 to 1.5
- attn_gain: float32 [2560], replicated, may hold values from 0.5 to 1.5
- w_x: bfloat16 [2560, 2560], P(('batch', 'seq')), may hold values from -0.125 to 0.125
- conv_w: float32 [4, 2560], replicated, may hold values from -3 to 3
- w_a: bfloat16 [10, 256, 256], replicated, may hold values from -0.375 to 0.375
- w_i: bfloat16 [10, 256, 256], replicated, may hold values from -0.375 to 0.375
- lru_decay: float32 [2560], replicated, may hold values from 4 to 20
- w_kv: bfloat16 [2560, 512], replicated, may hold values from -0.125 to 0.125
Outputs:
- lru_state: float32 [32, 2560], P('batch', 'seq')
- conv_state: bfloat16 [32, 3, 2560], P('batch', None, 'seq')
- kv_cache: bfloat16 [32, 2048, 512], P('batch', None, 'seq')
Inputs may be any that keep to these rules, and one draw needn't show every extreme that they name: `lengths`: positions from a prompt's length on are padding.
All inputs are finite; a program needn't handle non-finite values.
Results may differ from a plain program's by a relative error of at most 0.0051.
Values may be sent and summed in bfloat16 or wider, within the bound.
A program may use at most 128 MiB of HBM per device.

v0:
```python
import heapq

import jax
import jax.numpy as jnp
import numpy as np
from jax import lax
from jax.experimental import pallas as pl
from jax.experimental.pallas import tpu as pltpu
from jax.sharding import Mesh
from jax.sharding import PartitionSpec as P

HD = 256
W = 2048
SEQ = ("seq_0", "seq_1")
BATCH = ("batch_0", "batch_1", "batch_2")
BATCH_SEQ = BATCH + SEQ
MESH_ID = pl.DeviceIdType.MESH

RING = {"x": 4, "y": 4, "z": 8}
PLANS = ((0, 5, "xyz"), (5, 4, "zxy"), (9, 4, "zyx"))
HEADS = 5
COLS = HEADS * HD
WIDE = 13 * 128
MAIN = 2048
LEFT = 512
HALO = 16


def phase_copies(share, phase):
    size = RING[PLANS[share][2][phase]]
    copies = []
    for step in range(size // 2):
        for way in (1, -1):
            for half in (0, 1):
                if step < size // 2 - 1 or half == (way < 0):
                    copies.append((share, phase, way, step, half))
    return copies


def gather_schedule():
    copies = [c for s in range(3) for p in range(3) for c in phase_copies(s, p)]
    index = {c: k for k, c in enumerate(copies)}
    waiting = {}
    for c in copies:
        share, phase, way, step, half = c
        if step:
            waiting[c] = {(share, phase, way, step - 1, half)}
        else:
            waiting[c] = set(phase_copies(share, phase - 1)) if phase else set()
    free, arrivals, order = {}, [], []

    def send(c, now):
        share, phase, way, _, _ = c
        volume = PLANS[share][1]
        for dim in PLANS[share][2][:phase]:
            volume *= RING[dim]
        link = (PLANS[share][2][phase], way)
        free[link] = max(now, free.get(link, 0.0)) + volume * 2048 / 46.6e3
        heapq.heappush(arrivals, (free[link] + 1.8, index[c]))
        order.append(("send", index[c], now))

    for c in copies:
        if not waiting[c]:
            send(c, 0.0)
    while arrivals:
        now, k = heapq.heappop(arrivals)
        order.append(("recv", k, now))
        for c in copies:
            if copies[k] in waiting[c]:
                waiting[c].discard(copies[k])
                if not waiting[c]:
                    send(c, now)
    return copies, order


COPIES, ORDER = gather_schedule()


def column_orders():
    order = np.zeros((640, 640), np.float32)
    for q in range(64):
        x, core, y, z_hi = q // 16, q // 8 % 2, q // 2 % 4, q % 2
        spot = x * 8 + y * 2 + core
        for i in range(10):
            if i < 8:
                order[10 * q + i, z_hi * 256 + spot * 8 + i] = 1
            else:
                order[10 * q + i, 512 + (i - 8) * 64 + z_hi * 32 + spot] = 1
    sort = np.zeros((256, 256), np.float32)
    for row in range(256):
        sort[row, row % 32 * 8 + row // 32] = 1
    return jnp.asarray(order, jnp.bfloat16), jnp.asarray(sort, jnp.bfloat16)


def f32_dot(a, b):
    return jnp.dot(a, b, preferred_element_type=jnp.float32)


def normed_rows(raw, gain):
    wide = raw.astype(jnp.float32)
    inverse = lax.rsqrt(jnp.mean(wide * wide, axis=-1, keepdims=True) + 1e-06)
    return (wide * inverse * gain).astype(jnp.bfloat16)


def sigmoid(values):
    return 1.0 / (1.0 + jnp.exp(-values))


def prefill_kernel(
    block_hbm,
    tokens_hbm,
    attn_hbm,
    wkv_hbm,
    wa_hbm,
    wi_hbm,
    tail_ref,
    length_ref,
    gain_ref,
    attn_gain_ref,
    order_ref,
    sort_ref,
    conv_ref,
    rate_ref,
    cos_ref,
    sin_ref,
    state_out,
    conv_out,
    cache_out,
    wide,
    rows,
    ordered,
    left,
    proj,
    gate_in,
    attn,
    wkv,
    gates,
    halo,
    other_length,
    sums,
    parts,
    arrived,
    packed,
    cached,
    send_sem,
    recv_sem,
    pair_send,
    pair_recv,
    local_sem,
    part_send,
    part_recv,
    kv_send,
    kv_recv,
):
    z_lo = lax.axis_index("batch_0")
    core = lax.axis_index("batch_2")
    z_hi = lax.axis_index("seq_1")
    me = {"x": lax.axis_index("batch_1"), "y": lax.axis_index("seq_0"), "z": z_hi * 4 + z_lo}
    place = me["y"] * 2 + z_hi
    local_len = tokens_hbm.shape[0]
    span = HALO + local_len

    def toward(dim, way):
        spot = lax.rem(me[dim] + way + RING[dim], RING[dim])
        if dim == "x":
            return {"batch_1": spot}
        if dim == "y":
            return {"seq_0": spot}
        return {"batch_0": lax.rem(spot, 4), "seq_1": spot // 4}

    def beside(spot, c):
        return {"batch_2": c, "seq_0": spot // 2, "seq_1": lax.rem(spot, 2)}

    partner = {"batch_2": 1 - core}
    after = beside(lax.rem(place + 1, 8), core)

    barrier = pltpu.get_barrier_semaphore()
    friends = [toward(d, w) for d in "xz" for w in (1, -1)]
    for turn in range(8):
        for flip in range(2):
            if turn or flip:
                friends.append(beside(lax.rem(place + turn, 8), lax.rem(core + flip, 2)))
    for friend in friends:
        pl.semaphore_signal(barrier, inc=1, device_id=friend, device_id_type=MESH_ID)

    def remote(src, dst, sems, k, device):
        return pltpu.make_async_remote_copy(
            src_ref=src,
            dst_ref=dst,
            send_sem=sems[0].at[k],
            recv_sem=sems[1].at[k],
            device_id=device,
            device_id_type=MESH_ID,
        )

    mine = wide.at[me["z"], me["x"], pl.ds(2 * me["y"] + core, 1)]
    own_heads = pl.ds(HEADS * core, HEADS)
    fetches = [
        pltpu.make_async_copy(src, dst, local_sem.at[k])
        for k, (src, dst) in enumerate(
            (
                (tokens_hbm, rows.at[0]),
                (block_hbm.at[pl.ds(core, 1)], mine),
                (attn_hbm, attn),
                (wkv_hbm, wkv),
                (wa_hbm.at[own_heads], gates.at[0]),
                (wi_hbm.at[own_heads], gates.at[1]),
            )
        )
    ]
    for fetch in fetches:
        fetch.start()

    def place_rows(slot, start, raw):
        normed = normed_rows(raw, gain_ref[...])
        at = pl.ds(slot * span + start, raw.shape[0])
        for g in range(4):
            moved = f32_dot(normed[:, 640 * g : 640 * (g + 1)], order_ref[...])
            moved = moved.astype(jnp.bfloat16)
            ordered[at, pl.ds(256 * g, 256)] = moved[:, :256]
            ordered[at, pl.ds(1024 + 256 * g, 256)] = moved[:, 256:512]
            ordered[at, pl.ds(MAIN + 128 * g, 128)] = moved[:, 512:]

    def body_rows(slot, k):
        place_rows(slot, HALO + 256 * k, rows[slot, 256 * k : 256 * (k + 1), :])

    def edge_rows(slot):
        edge = halo[slot].astype(jnp.float32)
        blank = jnp.zeros((HALO - 4, edge.shape[1]), jnp.float32)
        place_rows(slot, 0, jnp.concatenate([blank, edge], axis=0))

    length = length_ref[0:1, 0:1]

    def cache_rows(k):
        tops = []
        lane = lax.broadcasted_iota(jnp.int32, (128, 128), 1)
        for start in (128 * k, 256 + 128 * k):
            normed = normed_rows(attn[start : start + 128, :], attn_gain_ref[...])
            kv = f32_dot(normed, wkv[...])
            turned = kv[:, :128] * cos_ref[start : start + 128, :]
            turned = turned + pltpu.roll(kv[:, :128], 64, 1) * sin_ref[start : start + 128, :]
            kv = jnp.concatenate([turned, kv[:, 128:]], axis=1).astype(jnp.bfloat16)
            at = place * local_len + start + lax.broadcasted_iota(jnp.int32, (128, 1), 0)
            inside = ((at >= length - W) & (at < length)).astype(jnp.float32)
            tops.append(kv.astype(jnp.float32) * inside)
        for t in range(4):
            upper = tops[0][:, 128 * t : 128 * (t + 1)]
            lower = tops[1][:, 128 * t : 128 * (t + 1)]
            even = jnp.where(lane < 64, upper, pltpu.roll(lower, 64, 1))
            odd = jnp.where(lane < 64, pltpu.roll(upper, 64, 1), lower)
            packed[2 * t, 128 * k : 128 * (k + 1), :] = even.astype(jnp.bfloat16)
            packed[2 * t + 1, 128 * k : 128 * (k + 1), :] = odd.astype(jnp.bfloat16)

    fetches[0].wait()
    body_rows(0, 0)
    pl.semaphore_wait(barrier, len(friends))

    pair = (pair_send, pair_recv)
    given = remote(block_hbm.at[pl.ds(1 - core, 1)], mine, pair, 0, partner)
    given.start()
    tail = remote(tail_ref, halo.at[0], pair, 1, after)
    tail.start()
    length_copy = remote(length_ref, other_length, pair, 2, partner)
    length_copy.start()
    rows_copy = remote(tokens_hbm, rows.at[1], pair, 3, partner)
    rows_copy.start()
    passed = remote(halo.at[0], halo.at[1], pair, 4, partner)

    def gather_copy(k):
        share, phase, way, step, half = COPIES[k]
        first, count, order = PLANS[share]
        dim = order[phase]
        spans = {d: pl.ds(0, RING[d]) for d in order[:phase]}
        spot = lax.rem(me[dim] - way * step + RING[dim], RING[dim])
        spans[dim] = pl.ds(spot, 1)
        for d in order[phase + 1 :]:
            spans[d] = pl.ds(me[d], 1)
        if "y" in order[:phase]:
            spans["y"] = pl.ds(4 * half, 4)
        else:
            y_at = spot if dim == "y" else me["y"]
            spans["y"] = pl.ds(2 * y_at + half, 1)
        piece = wide.at[
            spans["z"], spans["x"], spans["y"], pl.ds(0, 8), pl.ds(first * 128, count * 128)
        ]
        return remote(piece, piece, (send_sem, recv_sem), k, toward(dim, way))

    def start_other():
        rows_copy.wait()
        body_rows(1, 0)

    def pass_halo():
        tail.wait()
        passed.start()

    def start_cache():
        fetches[2].wait()
        fetches[3].wait()
        cache_rows(0)

    def end_halo():
        passed.wait()
        edge_rows(1)

    tasks = [
        (6.0, pass_halo),
        (10.0, lambda: body_rows(0, 1)),
        (14.0, start_other),
        (17.0, lambda: body_rows(1, 1)),
        (20.0, start_cache),
        (23.0, lambda: cache_rows(1)),
        (26.0, lambda: edge_rows(0)),
        (28.0, end_halo),
    ]
    fetches[1].wait()
    given.wait()
    started = {}
    for what, k, when in ORDER:
        if what == "send":
            started[k] = gather_copy(k)
            started[k].start()
        else:
            while tasks and tasks[0][0] <= when:
                tasks.pop(0)[1]()
            started[k].wait_recv()
    for _, task in tasks:
        task()

    def kv_copy(turn):
        spot = lax.rem(place + turn, 8)
        return pltpu.make_async_remote_copy(
            src_ref=packed.at[spot],
            dst_ref=cached.at[place],
            send_sem=kv_send.at[turn],
            recv_sem=kv_recv.at[turn],
            device_id=beside(spot, core),
            device_id_type=MESH_ID,
        )

    kv_copies = [kv_copy(turn) for turn in range(1, 8)]
    for copy in kv_copies:
        copy.start()
    fetches[4].wait()
    fetches[5].wait()
    length_copy.wait()

    for z in range(8):
        rest = wide[z, :, :, :, COLS:].reshape(256, WIDE - COLS)
        sorted_rows = f32_dot(sort_ref[...], rest).astype(jnp.bfloat16)
        for r in range(2):
            for j in range(10):
                unit = r * 10 + j
                row = z % 4 * 128 + r * 64 + z // 4 * 32
                left[row : row + 32, 128 * j : 128 * (j + 1)] = sorted_rows[
                    32 * (unit % 8) : 32 * (unit % 8) + 32,
                    128 * (unit // 8) : 128 * (unit // 8 + 1),
                ]

    later_rows = (
        lax.broadcasted_iota(jnp.int32, (256, 256), 1)
        > lax.broadcasted_iota(jnp.int32, (256, 256), 0)
    ).astype(jnp.bfloat16)
    lengths = (length, other_length[0:1, 0:1])

    def head_step(head, carry):
        columns = pl.ds(pl.multiple_of(head * HD, HD), HD)
        channels = pl.ds(pl.multiple_of((HEADS * core + head) * HD, HD), HD)
        weight = wide[:, :, :, :, columns].reshape(MAIN, HD)
        total = f32_dot(ordered[:, :MAIN], weight)
        total = total + f32_dot(ordered[:, MAIN:], left[:, columns])
        proj[...] = total.astype(jnp.bfloat16).astype(jnp.float32)
        taps = conv_ref[:, channels]
        rate = rate_ref[:, channels]
        for slot in range(2):
            base = slot * span
            edge = proj[base : base + HALO, :]
            proj[base : base + HALO, :] = jnp.where(place > 0, edge, 0.0)
            spots = place * local_len + lax.broadcasted_iota(jnp.int32, (8, local_len), 1)
            wanted = lengths[slot] - 3 + lax.broadcasted_iota(jnp.int32, (8, local_len), 0)
            picker = (spots == wanted).astype(jnp.bfloat16)
            picked = f32_dot(picker, proj[base + HALO : base + span, :].astype(jnp.bfloat16))
            log_total = jnp.zeros((1, HD), jnp.float32)
            state = jnp.zeros((1, HD), jnp.float32)
            for part in range(local_len // 256):
                first = base + HALO - 3 + 256 * part
                conv_sum = taps[0:1, :] * proj[pl.ds(first, 256), :]
                for offset in range(1, 4):
                    tap = taps[offset : offset + 1, :]
                    conv_sum = conv_sum + tap * proj[pl.ds(first + offset, 256), :]
                x_conv = conv_sum.astype(jnp.bfloat16)
                gate_a = f32_dot(x_conv, gates[0, head])
                gate_i = f32_dot(x_conv, gates[1, head])
                at = place * local_len + 256 * part
                at = at + lax.broadcasted_iota(jnp.int32, (256, 1), 0)
                valid = (at < lengths[slot]).astype(jnp.float32)
                log_rate = rate * sigmoid(gate_a)
                y = 2.0 * log_rate
                series = 1.0 / 720.0 + y * (1.0 / 5040.0)
                for c in (1.0 / 120.0, 1.0 / 24.0, 1.0 / 6.0, 0.5, 1.0):
                    series = c + y * series
                push = jnp.sqrt(-y * series) * sigmoid(gate_i)
                push = push * x_conv.astype(jnp.float32) * valid
                kept = log_rate * valid
                high = kept.astype(jnp.bfloat16)
                low = (kept - high.astype(jnp.float32)).astype(jnp.bfloat16)
                later = f32_dot(later_rows, high) + f32_dot(later_rows, low)
                add = jnp.sum(jnp.exp(later) * push, axis=0, keepdims=True)
                log_part = jnp.sum(kept, axis=0, keepdims=True)
                state = jnp.exp(log_part) * state + add
                log_total = log_total + log_part
            sums[slot, 0:1, columns] = log_total
            sums[slot, 1:2, columns] = state
            sums[slot, 2:5, columns] = picked[0:3]
        return carry

    sums[...] = jnp.zeros_like(sums)
    lax.fori_loop(0, HEADS, head_step, 0)

    for slot in range(2):
        for k in range(4):
            whole = sums[slot]
            if k:
                whole = pltpu.roll(whole, COLS - 320 * k, 1)
            parts[slot, k] = whole[:, :384]

    def part_copy(slot, k):
        return pltpu.make_async_remote_copy(
            src_ref=parts.at[slot, k],
            dst_ref=arrived.at[place],
            send_sem=part_send.at[slot * 4 + k],
            recv_sem=part_recv.at[place],
            device_id=beside(4 * core + k, lax.rem(core + slot, 2)),
            device_id_type=MESH_ID,
        )

    def is_own(slot, k):
        return jnp.logical_and(slot == 0, place == 4 * core + k)

    for slot in range(2):
        for k in range(4):

            @pl.when(jnp.logical_not(is_own(slot, k)))
            def _(slot=slot, k=k):
                part_copy(slot, k).start()

    for k in range(4):

        @pl.when(is_own(0, k))
        def _(k=k):
            arrived[place] = parts[0, k]

    cached[place] = packed[place]
    for copy in kv_copies:
        copy.wait()
    for k in range(4):
        both = cached[k].astype(jnp.float32) + cached[k + 4].astype(jnp.float32)
        cache_out[512 * k : 512 * k + 256, :] = both[:, :64].astype(jnp.bfloat16)
        turned = pltpu.roll(both, 64, 1)
        cache_out[512 * k + 256 : 512 * k + 512, :] = turned[:, :64].astype(jnp.bfloat16)

    near = core == place // 4
    for spot in range(8):

        @pl.when(jnp.logical_not(jnp.logical_and(near, place == spot)))
        def _(spot=spot):
            pltpu.make_async_remote_copy(
                src_ref=parts.at[0, 0],
                dst_ref=arrived.at[spot],
                send_sem=part_send.at[0],
                recv_sem=part_recv.at[spot],
                device_id=partner,
                device_id_type=MESH_ID,
            ).wait_recv()

    width = state_out.shape[1]
    state = jnp.zeros((1, width), jnp.float32)
    conv = jnp.zeros((3, width), jnp.float32)
    for spot in range(8):
        state = jnp.exp(arrived[spot, 0:1, :width]) * state + arrived[spot, 1:2, :width]
        conv = conv + arrived[spot, 2:5, :width]
    state_out[...] = state
    conv_out[...] = conv.astype(jnp.bfloat16)
    for slot in range(2):
        for k in range(4):

            @pl.when(jnp.logical_not(is_own(slot, k)))
            def _(slot=slot, k=k):
                part_copy(slot, k).wait_send()

    for k in sorted(started):
        started[k].wait_send()


def prefill(block, tokens, attn_in, w_kv, w_a, w_i, *small):
    order, sort = column_orders()
    local_len, feature_dim = tokens.shape
    tail, length, gain, attn_gain, conv_w, rate, cosine, sine = small
    vmem = pl.BlockSpec(memory_space=pltpu.VMEM)
    hbm = pl.BlockSpec(memory_space=pl.ANY)
    dma = pltpu.SemaphoreType.DMA
    span = HALO + local_len
    return pl.pallas_call(
        prefill_kernel,
        out_shape=(
            jax.ShapeDtypeStruct((1, feature_dim // 8), jnp.float32),
            jax.ShapeDtypeStruct((3, feature_dim // 8), jnp.bfloat16),
            jax.ShapeDtypeStruct((W, 64), jnp.bfloat16),
        ),
        in_specs=[hbm] * 6 + [vmem] * 10,
        out_specs=(vmem, vmem, vmem),
        scratch_shapes=[
            pltpu.VMEM((8, 4, 8, 8, WIDE), jnp.bfloat16),
            pltpu.VMEM((2, local_len, feature_dim), jnp.bfloat16),
            pltpu.VMEM((2 * span, feature_dim), jnp.bfloat16),
            pltpu.VMEM((LEFT, COLS), jnp.bfloat16),
            pltpu.VMEM((2 * span, HD), jnp.float32),
            pltpu.VMEM((local_len, HD), jnp.bfloat16),
            pltpu.VMEM((local_len, feature_dim), jnp.bfloat16),
            pltpu.VMEM(w_kv.shape, jnp.bfloat16),
            pltpu.VMEM((2, HEADS, HD, HD), jnp.bfloat16),
            pltpu.VMEM((2, 4, feature_dim), jnp.bfloat16),
            pltpu.VMEM((8, 128), jnp.int32),
            pltpu.VMEM((2, 8, COLS), jnp.float32),
            pltpu.VMEM((2, 4, 8, 384), jnp.float32),
            pltpu.VMEM((8, 8, 384), jnp.float32),
            pltpu.VMEM((8, local_len // 2, 128), jnp.bfloat16),
            pltpu.VMEM((8, local_len // 2, 128), jnp.bfloat16),
            dma((len(COPIES),)),
            dma((len(COPIES),)),
            dma((5,)),
            dma((5,)),
            dma((6,)),
            dma((8,)),
            dma((8,)),
            dma((8,)),
            dma((8,)),
        ],
        compiler_params=pltpu.CompilerParams(
            collective_id=0, has_side_effects=True, vmem_limit_bytes=63 * 2**20
        ),
    )(
        block, tokens, attn_in, w_kv, w_a, w_i, tail, length, gain, attn_gain, order, sort,
        conv_w, rate, cosine, sine,
    )


def transport_block(w_rows):
    halves = w_rows.reshape(10, 2, COLS).transpose(1, 0, 2)
    rest = halves[:, 8:].reshape(2, 20, 128)
    rest = jnp.concatenate([rest, jnp.zeros((2, 4, 128), rest.dtype)], axis=1)
    rest = rest.reshape(2, 3, 8, 128).transpose(0, 2, 1, 3).reshape(2, 8, 384)
    return jnp.concatenate([halves[:, :8], rest], axis=2)


def on_device(
    tokens, attn_in, lengths, norm_gain, attn_gain, w_x, conv_w, w_a, w_i, lru_decay, w_kv
):
    local_len = tokens.shape[1]
    place = lax.axis_index(SEQ)
    positions = place * local_len + jnp.arange(local_len, dtype=jnp.int32)
    spacing = jnp.exp(-jnp.log(10000.0) * jnp.arange(64, dtype=jnp.float32) / 64)
    angles = positions.astype(jnp.float32)[:, None] * spacing[None, :]
    cosine, sine = jnp.cos(angles), jnp.sin(angles)
    lru_state, conv_state, kv_cache = prefill(
        transport_block(w_x),
        tokens[0],
        attn_in[0],
        w_kv,
        w_a,
        w_i,
        tokens[0, local_len - 4 :],
        jnp.broadcast_to(lengths[0], (8, 128)),
        norm_gain[None],
        attn_gain[None],
        conv_w,
        (-8.0 * jax.nn.softplus(-lru_decay))[None],
        jnp.concatenate([cosine, cosine], axis=1),
        jnp.concatenate([-sine, sine], axis=1),
    )
    return (lru_state, conv_state[None], kv_cache[None])


def solution(mesh):
    split = Mesh(mesh.devices.reshape(4, 4, 2, 4, 2), BATCH_SEQ)
    in_specs = (
        P(BATCH, SEQ, None),
        P(BATCH, SEQ, None),
        P(BATCH),
        P(),
        P(),
        P(BATCH_SEQ, None),
        P(),
        P(),
        P(),
        P(),
        P(),
    )
    out_specs = (P(BATCH, SEQ), P(BATCH, None, SEQ), P(BATCH, None, SEQ))
    return jax.shard_map(
        on_device, mesh=split, in_specs=in_specs, out_specs=out_specs, check_vma=False
    )
```

profile of v0, /device:TPU:33, one launch (start us, length us, event | category | flops | bytes accessed | tf_op | source)
XLA Modules:
  0.0 110.1 jit_solution(7121121762254725973)
XLA Ops:
  0.6 0.0 copy-start
  0.6 0.0 copy-start.1
  0.7 0.0 copy-start.2
  0.7 1.0 fusion
  1.7 1.0 pad_maximum_fusion
  2.7 0.9 reshape.28
  3.7 0.6 pad_maximum_fusion.2.block_hbm
  4.3 0.0 copy-done
  4.3 0.6 broadcast_in_dim.24.rate_ref
  4.9 1.4 %slice_bitcast_fusion.tail_ref = bf16[4,2560]{1,0:T(4,128)(2,1)} fusion(bf16[1,512,2560]{2,1,0:T(8,128)(2,1)} %param.13), kind=kLoop, calls=%fused_computation.8 | loop fusion | bytes 40960 | tf_op jit(solution)/shard_map/squeeze | solution.py:571
  6.3 0.0 copy-done.1
  6.3 0.6 broadcast_in_dim.22.gain_ref
  6.9 0.0 copy-done.2
  6.9 0.6 broadcast_in_dim.23.attn_gain_ref
  8.2 0.6 broadcast_in_dim.21.length_ref
  8.8 96.9 %shard_map.148 = (f32[1,320]{1,0:T(1,128)}, bf16[3,320]{1,0:T(4,128)(2,1)}, bf16[2048,64]{1,0:T(8,128)(2,1)}) custom-call(bf16[2,8,1664]{2,1,0:T(8,128)(2,1)} %pad_maximum_fusion.2.block_hbm, bf16[512,2560]{1,0:T(8,128)(2,1)} %bitcast.17, bf16[512,2560]{1,0:T(8,128)(2,1)} %bitcast.18, bf16[2560,512]{1,0:T(8,128)(2,1)} %wkv_hbm.1, ...), custom_call_target="tpu_custom_call" | custom-call | tf_op jit(solution)/shard_map/pallas_call | solution.py:502
  105.7 1.9 %copy.18 = bf16[1,2048,64]{1,2,0:T(8,128)(2,1)} copy(bf16[1,2048,64]{2,1,0:T(8,128)(2,1)} %bitcast.19) | data formatting | bytes 524288
  107.6 1.2 %copy.24 = f32[1,320]{1,0:T(1,128)} copy(f32[1,320]{1,0:T(1,128)} %get-tuple-element.23) | data formatting | bytes 2560
  108.9 1.3 %copy.25 = bf16[1,3,320]{2,1,0:T(4,128)(2,1)} copy(bf16[1,3,320]{2,1,0:T(4,128)(2,1)} %bitcast.22) | data formatting | bytes 3840
  (8 shorter events, 0.1 us)
Async XLA Ops:
  0.6 3.7 %copy-start = (f32[2560]{0:T(1024)S(1)}, f32[2560]{0:T(1024)}, u32[]{:S(2)}) copy-start(f32[2560]{0:T(1024)} %param.22) | copy-start | bytes 30724
  0.6 5.7 %copy-start.1 = (f32[2560]{0:T(1024)S(1)}, f32[2560]{0:T(1024)}, u32[]{:S(2)}) copy-start(f32[2560]{0:T(1024)} %param.16) | copy-start | bytes 30724
  0.7 6.3 %copy-start.2 = (f32[2560]{0:T(1024)S(1)}, f32[2560]{0:T(1024)}, u32[]{:S(2)}) copy-start(f32[2560]{0:T(1024)} %param.17) | copy-start | bytes 30724
where the time goes:
time: 110 us
  Pallas kernels  96.9 us (88%)
  local copies, waits for them, and re-layouts  9.19 us (8%)
  other arithmetic  2.63 us (2%)
  between operations  1.39 us (1%)
    pallas_call x1, Pallas kernels, prefill(): pl.pallas_call(prefill_kernel, out_shape=(jax.ShapeDtypeStruct((1, featur...  96.9 us
    unnamed x9, local copies, waits for them, and re-layouts  4.44 us

commit v1 on v0

--- a/solution.py
+++ b/solution.py
@@ -107,41 +107,40 @@
 
 
 def prefill_kernel(
-    block_hbm,
+    length_in,
     tokens_hbm,
     attn_hbm,
     wkv_hbm,
     wa_hbm,
     wi_hbm,
-    tail_ref,
-    length_ref,
+    shard_ref,
     gain_ref,
     attn_gain_ref,
+    decay_ref,
+    conv_ref,
     order_ref,
     sort_ref,
-    conv_ref,
-    rate_ref,
-    cos_ref,
-    sin_ref,
-    state_out,
-    conv_out,
-    cache_out,
+    trig_ref,
+    arrived,
+    cached,
     wide,
     rows,
     ordered,
     left,
-    proj,
-    gate_in,
+    proj_even,
+    proj_odd,
     attn,
     wkv,
     gates,
     halo,
-    other_length,
+    tail_rows,
+    lengths_ref,
+    block,
+    rest_tiles,
+    fall,
     sums,
     parts,
-    arrived,
     packed,
-    cached,
     send_sem,
     recv_sem,
     pair_send,
@@ -193,14 +192,13 @@
             device_id_type=MESH_ID,
         )
 
-    mine = wide.at[me["z"], me["x"], pl.ds(2 * me["y"] + core, 1)]
+    mine = (me["z"], me["x"], pl.ds(2 * me["y"] + core, 1))
     own_heads = pl.ds(HEADS * core, HEADS)
     fetches = [
         pltpu.make_async_copy(src, dst, local_sem.at[k])
         for k, (src, dst) in enumerate(
             (
                 (tokens_hbm, rows.at[0]),
-                (block_hbm.at[pl.ds(core, 1)], mine),
                 (attn_hbm, attn),
                 (wkv_hbm, wkv),
                 (wa_hbm.at[own_heads], gates.at[0]),
@@ -211,6 +209,26 @@
     for fetch in fetches:
         fetch.start()
 
+    shard = shard_ref[...].astype(jnp.float32)
+    rest_tiles[...] = jnp.zeros_like(rest_tiles)
+    for side in range(2):
+        for unit in range(20):
+            r, j = unit // 10, unit % 10
+            column = COLS * side + 128 * j
+            tile = 128 * (unit // 8)
+            rest_tiles[side, unit % 8 : unit % 8 + 1, tile : tile + 128] = shard[
+                8 + r : 9 + r, column : column + 128
+            ]
+        block[side, :, :COLS] = shard[:8, COLS * side : COLS * (side + 1)].astype(jnp.bfloat16)
+        block[side, :, COLS:] = rest_tiles[side].astype(jnp.bfloat16)
+    wide[mine] = block[pl.ds(core, 1)]
+    lengths_ref[0] = jnp.full((8, 128), length_in[0], jnp.int32)
+    spread = jnp.exp(-decay_ref[...])
+    series = 1.0 / 5.0 - spread * (1.0 / 6.0)
+    for c in (1.0 / 4.0, 1.0 / 3.0, 0.5, 1.0):
+        series = c - spread * series
+    fall[...] = (8.0 * spread) * series
+
     def place_rows(slot, start, raw):
         normed = normed_rows(raw, gain_ref[...])
         at = pl.ds(slot * span + start, raw.shape[0])
@@ -229,7 +247,15 @@
         blank = jnp.zeros((HALO - 4, edge.shape[1]), jnp.float32)
         place_rows(slot, 0, jnp.concatenate([blank, edge], axis=0))
 
-    length = length_ref[0:1, 0:1]
+    length = lengths_ref[0, 0:1, 0:1]
+
+    def rotation(start):
+        cosines, sines = [], []
+        for lap in (start // 64, start // 64 + 1):
+            at = pl.ds(place * (local_len // 64) + lap, 1)
+            cosines.append(trig_ref[0, at, :] * trig_ref[2] - trig_ref[1, at, :] * trig_ref[3])
+            sines.append(trig_ref[1, at, :] * trig_ref[2] + trig_ref[0, at, :] * trig_ref[3])
+        return jnp.concatenate(cosines, axis=0), jnp.concatenate(sines, axis=0)
 
     def cache_rows(k):
         tops = []
@@ -237,8 +263,8 @@
         for start in (128 * k, 256 + 128 * k):
             normed = normed_rows(attn[start : start + 128, :], attn_gain_ref[...])
             kv = f32_dot(normed, wkv[...])
-            turned = kv[:, :128] * cos_ref[start : start + 128, :]
-            turned = turned + pltpu.roll(kv[:, :128], 64, 1) * sin_ref[start : start + 128, :]
+            cosine, sine = rotation(start)
+            turned = kv[:, :128] * cosine + pltpu.roll(kv[:, :128], 64, 1) * sine
             kv = jnp.concatenate([turned, kv[:, 128:]], axis=1).astype(jnp.bfloat16)
             at = place * local_len + start + lax.broadcasted_iota(jnp.int32, (128, 1), 0)
             inside = ((at >= length - W) & (at < length)).astype(jnp.float32)
@@ -251,16 +277,13 @@
             packed[2 * t, 128 * k : 128 * (k + 1), :] = even.astype(jnp.bfloat16)
             packed[2 * t + 1, 128 * k : 128 * (k + 1), :] = odd.astype(jnp.bfloat16)
 
-    fetches[0].wait()
-    body_rows(0, 0)
     pl.semaphore_wait(barrier, len(friends))
 
     pair = (pair_send, pair_recv)
-    given = remote(block_hbm.at[pl.ds(1 - core, 1)], mine, pair, 0, partner)
+    given = remote(block.at[pl.ds(1 - core, 1)], wide.at[mine], pair, 0, partner)
     given.start()
-    tail = remote(tail_ref, halo.at[0], pair, 1, after)
-    tail.start()
-    length_copy = remote(length_ref, other_length, pair, 2, partner)
+    tail = remote(tail_rows, halo.at[0], pair, 1, after)
+    length_copy = remote(lengths_ref.at[0], lengths_ref.at[1], pair, 2, partner)
     length_copy.start()
     rows_copy = remote(tokens_hbm, rows.at[1], pair, 3, partner)
     rows_copy.start()
@@ -285,6 +308,13 @@
         ]
         return remote(piece, piece, (send_sem, recv_sem), k, toward(dim, way))
 
+    def start_own():
+        fetches[0].wait()
+        last = rows[0, local_len - 8 :, :].astype(jnp.float32)
+        tail_rows[...] = last[4:].astype(jnp.bfloat16)
+        body_rows(0, 0)
+        tail.start()
+
     def start_other():
         rows_copy.wait()
         body_rows(1, 0)
@@ -292,10 +322,11 @@
     def pass_halo():
         tail.wait()
         passed.start()
+        edge_rows(0)
 
     def start_cache():
+        fetches[1].wait()
         fetches[2].wait()
-        fetches[3].wait()
         cache_rows(0)
 
     def end_halo():
@@ -303,16 +334,15 @@
         edge_rows(1)
 
     tasks = [
-        (6.0, pass_halo),
+        (0.0, start_own),
         (10.0, lambda: body_rows(0, 1)),
-        (14.0, start_other),
-        (17.0, lambda: body_rows(1, 1)),
-        (20.0, start_cache),
-        (23.0, lambda: cache_rows(1)),
-        (26.0, lambda: edge_rows(0)),
+        (14.0, pass_halo),
+        (16.0, start_other),
+        (19.0, lambda: body_rows(1, 1)),
+        (22.0, start_cache),
+        (25.0, lambda: cache_rows(1)),
         (28.0, end_halo),
     ]
-    fetches[1].wait()
     given.wait()
     started = {}
     for what, k, when in ORDER:
@@ -340,8 +370,10 @@
     kv_copies = [kv_copy(turn) for turn in range(1, 8)]
     for copy in kv_copies:
         copy.start()
+    local = pltpu.make_async_copy(packed.at[place], cached.at[place], local_sem.at[5])
+    local.start()
+    fetches[3].wait()
     fetches[4].wait()
-    fetches[5].wait()
     length_copy.wait()
 
     for z in range(8):
@@ -360,25 +392,28 @@
         lax.broadcasted_iota(jnp.int32, (256, 256), 1)
         > lax.broadcasted_iota(jnp.int32, (256, 256), 0)
     ).astype(jnp.bfloat16)
-    lengths = (length, other_length[0:1, 0:1])
-
-    def head_step(head, carry):
-        columns = pl.ds(pl.multiple_of(head * HD, HD), HD)
+    lengths = (length, lengths_ref[1, 0:1, 0:1])
+
+    def of_head(head):
+        return pl.ds(pl.multiple_of(head * HD, HD), HD)
+
+    def project(head, proj):
+        weight = wide[:, :, :, :, of_head(head)].reshape(MAIN, HD)
+        total = f32_dot(ordered[:, :MAIN], weight)
+        total = total + f32_dot(ordered[:, MAIN:], left[:, of_head(head)])
+        proj[...] = total.astype(jnp.bfloat16).astype(jnp.float32)
+
+    def fold(head, proj):
+        columns = of_head(head)
         channels = pl.ds(pl.multiple_of((HEADS * core + head) * HD, HD), HD)
-        weight = wide[:, :, :, :, columns].reshape(MAIN, HD)
-        total = f32_dot(ordered[:, :MAIN], weight)
-        total = total + f32_dot(ordered[:, MAIN:], left[:, columns])
-        proj[...] = total.astype(jnp.bfloat16).astype(jnp.float32)
         taps = conv_ref[:, channels]
-        rate = rate_ref[:, channels]
+        pace = fall[:, channels]
         for slot in range(2):
             base = slot * span
             edge = proj[base : base + HALO, :]
             proj[base : base + HALO, :] = jnp.where(place > 0, edge, 0.0)
-            spots = place * local_len + lax.broadcasted_iota(jnp.int32, (8, local_len), 1)
-            wanted = lengths[slot] - 3 + lax.broadcasted_iota(jnp.int32, (8, local_len), 0)
-            picker = (spots == wanted).astype(jnp.bfloat16)
-            picked = f32_dot(picker, proj[base + HALO : base + span, :].astype(jnp.bfloat16))
+        for slot in range(2):
+            base = slot * span
             log_total = jnp.zeros((1, HD), jnp.float32)
             state = jnp.zeros((1, HD), jnp.float32)
             for part in range(local_len // 256):
@@ -393,14 +428,12 @@
                 at = place * local_len + 256 * part
                 at = at + lax.broadcasted_iota(jnp.int32, (256, 1), 0)
                 valid = (at < lengths[slot]).astype(jnp.float32)
-                log_rate = rate * sigmoid(gate_a)
-                y = 2.0 * log_rate
-                series = 1.0 / 720.0 + y * (1.0 / 5040.0)
-                for c in (1.0 / 120.0, 1.0 / 24.0, 1.0 / 6.0, 0.5, 1.0):
-                    series = c + y * series
-                push = jnp.sqrt(-y * series) * sigmoid(gate_i)
-                push = push * x_conv.astype(jnp.float32) * valid
-                kept = log_rate * valid
+                drop = pace * sigmoid(gate_a)
+                t = jnp.tanh(drop)
+                twice = 2.0 * t
+                push = twice * lax.rsqrt(jnp.maximum(twice * (1.0 + t), 1e-37))
+                push = push * sigmoid(gate_i) * x_conv.astype(jnp.float32) * valid
+                kept = -drop * valid
                 high = kept.astype(jnp.bfloat16)
                 low = (kept - high.astype(jnp.float32)).astype(jnp.bfloat16)
                 later = f32_dot(later_rows, high) + f32_dot(later_rows, low)
@@ -408,13 +441,25 @@
                 log_part = jnp.sum(kept, axis=0, keepdims=True)
                 state = jnp.exp(log_part) * state + add
                 log_total = log_total + log_part
+            spots = place * local_len + lax.broadcasted_iota(jnp.int32, (8, local_len), 1)
+            wanted = lengths[slot] - 3 + lax.broadcasted_iota(jnp.int32, (8, local_len), 0)
+            picker = (spots == wanted).astype(jnp.bfloat16)
+            picked = f32_dot(picker, proj[base + HALO : base + span, :].astype(jnp.bfloat16))
             sums[slot, 0:1, columns] = log_total
             sums[slot, 1:2, columns] = state
             sums[slot, 2:5, columns] = picked[0:3]
+
+    def head_pair(k, carry):
+        project(2 * k + 1, proj_odd)
+        fold(2 * k, proj_even)
+        project(2 * k + 2, proj_even)
+        fold(2 * k + 1, proj_odd)
         return carry
 
     sums[...] = jnp.zeros_like(sums)
-    lax.fori_loop(0, HEADS, head_step, 0)
+    project(0, proj_even)
+    lax.fori_loop(0, HEADS // 2, head_pair, 0)
+    fold(HEADS - 1, proj_even)
 
     for slot in range(2):
         for k in range(4):
@@ -447,17 +492,13 @@
 
         @pl.when(is_own(0, k))
         def _(k=k):
-            arrived[place] = parts[0, k]
-
-    cached[place] = packed[place]
+            copy = pltpu.make_async_copy(parts.at[0, k], arrived.at[place], local_sem.at[6])
+            copy.start()
+            copy.wait()
+
+    local.wait()
     for copy in kv_copies:
         copy.wait()
-    for k in range(4):
-        both = cached[k].astype(jnp.float32) + cached[k + 4].astype(jnp.float32)
-        cache_out[512 * k : 512 * k + 256, :] = both[:, :64].astype(jnp.bfloat16)
-        turned = pltpu.roll(both, 64, 1)
-        cache_out[512 * k + 256 : 512 * k + 512, :] = turned[:, :64].astype(jnp.bfloat16)
-
     near = core == place // 4
     for spot in range(8):
 
@@ -472,6 +513,18 @@
                 device_id_type=MESH_ID,
             ).wait_recv()
 
+    for slot in range(2):
+        for k in range(4):
+
+            @pl.when(jnp.logical_not(is_own(slot, k)))
+            def _(slot=slot, k=k):
+                part_copy(slot, k).wait_send()
+
+    for k in sorted(started):
+        started[k].wait_send()
+
+
+def finish_kernel(arrived, cached, state_out, conv_out, cache_out):
     width = state_out.shape[1]
     state = jnp.zeros((1, width), jnp.float32)
     conv = jnp.zeros((3, width), jnp.float32)
@@ -480,56 +533,63 @@
         conv = conv + arrived[spot, 2:5, :width]
     state_out[...] = state
     conv_out[...] = conv.astype(jnp.bfloat16)
-    for slot in range(2):
-        for k in range(4):
-
-            @pl.when(jnp.logical_not(is_own(slot, k)))
-            def _(slot=slot, k=k):
-                part_copy(slot, k).wait_send()
-
-    for k in sorted(started):
-        started[k].wait_send()
-
-
-def prefill(block, tokens, attn_in, w_kv, w_a, w_i, *small):
+    half = cached.shape[1]
+    for k in range(4):
+        both = cached[k].astype(jnp.float32) + cached[k + 4].astype(jnp.float32)
+        turned = both.T.astype(jnp.bfloat16)
+        cache_out[:, 2 * half * k : 2 * half * k + half] = turned[:64]
+        cache_out[:, 2 * half * k + half : 2 * half * (k + 1)] = turned[64:]
+
+
+def rotation_tables():
+    spacing = 10000.0 ** (-np.arange(64) / 64)
+    tables = []
+    for step in (64, 1):
+        angles = step * np.arange(64)[:, None] * spacing[None, :]
+        tables.append(np.concatenate([np.cos(angles), np.cos(angles)], axis=1))
+        tables.append(np.concatenate([-np.sin(angles), np.sin(angles)], axis=1))
+    return jnp.asarray(np.stack(tables), jnp.float32)
+
+
+def prefill(length, tokens, attn_in, w_kv, w_a, w_i, shard, gain, attn_gain, decay, conv_w):
     order, sort = column_orders()
     local_len, feature_dim = tokens.shape
-    tail, length, gain, attn_gain, conv_w, rate, cosine, sine = small
     vmem = pl.BlockSpec(memory_space=pltpu.VMEM)
     hbm = pl.BlockSpec(memory_space=pl.ANY)
     dma = pltpu.SemaphoreType.DMA
     span = HALO + local_len
-    return pl.pallas_call(
+    arrived, cached = pl.pallas_call(
         prefill_kernel,
         out_shape=(
-            jax.ShapeDtypeStruct((1, feature_dim // 8), jnp.float32),
-            jax.ShapeDtypeStruct((3, feature_dim // 8), jnp.bfloat16),
-            jax.ShapeDtypeStruct((W, 64), jnp.bfloat16),
+            jax.ShapeDtypeStruct((8, 8, 384), jnp.float32),
+            jax.ShapeDtypeStruct((8, local_len // 2, 128), jnp.bfloat16),
         ),
-        in_specs=[hbm] * 6 + [vmem] * 10,
-        out_specs=(vmem, vmem, vmem),
+        in_specs=[pl.BlockSpec(memory_space=pltpu.SMEM)] + [hbm] * 5 + [vmem] * 8,
+        out_specs=(hbm, hbm),
         scratch_shapes=[
             pltpu.VMEM((8, 4, 8, 8, WIDE), jnp.bfloat16),
             pltpu.VMEM((2, local_len, feature_dim), jnp.bfloat16),
             pltpu.VMEM((2 * span, feature_dim), jnp.bfloat16),
             pltpu.VMEM((LEFT, COLS), jnp.bfloat16),
             pltpu.VMEM((2 * span, HD), jnp.float32),
-            pltpu.VMEM((local_len, HD), jnp.bfloat16),
+            pltpu.VMEM((2 * span, HD), jnp.float32),
             pltpu.VMEM((local_len, feature_dim), jnp.bfloat16),
             pltpu.VMEM(w_kv.shape, jnp.bfloat16),
             pltpu.VMEM((2, HEADS, HD, HD), jnp.bfloat16),
             pltpu.VMEM((2, 4, feature_dim), jnp.bfloat16),
-            pltpu.VMEM((8, 128), jnp.int32),
+            pltpu.VMEM((4, feature_dim), jnp.bfloat16),
+            pltpu.VMEM((2, 8, 128), jnp.int32),
+            pltpu.VMEM((2, 8, WIDE), jnp.bfloat16),
+            pltpu.VMEM((2, 8, WIDE - COLS), jnp.float32),
+            pltpu.VMEM((1, feature_dim), jnp.float32),
             pltpu.VMEM((2, 8, COLS), jnp.float32),
             pltpu.VMEM((2, 4, 8, 384), jnp.float32),
-            pltpu.VMEM((8, 8, 384), jnp.float32),
-            pltpu.VMEM((8, local_len // 2, 128), jnp.bfloat16),
             pltpu.VMEM((8, local_len // 2, 128), jnp.bfloat16),
             dma((len(COPIES),)),
             dma((len(COPIES),)),
             dma((5,)),
             dma((5,)),
-            dma((6,)),
+            dma((7,)),
             dma((8,)),
             dma((8,)),
             dma((8,)),
@@ -539,45 +599,38 @@
             collective_id=0, has_side_effects=True, vmem_limit_bytes=63 * 2**20
         ),
     )(
-        block, tokens, attn_in, w_kv, w_a, w_i, tail, length, gain, attn_gain, order, sort,
-        conv_w, rate, cosine, sine,
+        length, tokens, attn_in, w_kv, w_a, w_i, shard, gain, attn_gain, decay, conv_w,
+        order, sort, rotation_tables(),
     )
-
-
-def transport_block(w_rows):
-    halves = w_rows.reshape(10, 2, COLS).transpose(1, 0, 2)
-    rest = halves[:, 8:].reshape(2, 20, 128)
-    rest = jnp.concatenate([rest, jnp.zeros((2, 4, 128), rest.dtype)], axis=1)
-    rest = rest.reshape(2, 3, 8, 128).transpose(0, 2, 1, 3).reshape(2, 8, 384)
-    return jnp.concatenate([halves[:, :8], rest], axis=2)
+    return pl.pallas_call(
+        finish_kernel,
+        out_shape=(
+            jax.ShapeDtypeStruct((1, feature_dim // 8), jnp.float32),
+            jax.ShapeDtypeStruct((3, feature_dim // 8), jnp.bfloat16),
+            jax.ShapeDtypeStruct((64, W), jnp.bfloat16),
+        ),
+        in_specs=[vmem, vmem],
+        out_specs=(vmem, vmem, vmem),
+    )(arrived, cached)
 
 
 def on_device(
     tokens, attn_in, lengths, norm_gain, attn_gain, w_x, conv_w, w_a, w_i, lru_decay, w_kv
 ):
-    local_len = tokens.shape[1]
-    place = lax.axis_index(SEQ)
-    positions = place * local_len + jnp.arange(local_len, dtype=jnp.int32)
-    spacing = jnp.exp(-jnp.log(10000.0) * jnp.arange(64, dtype=jnp.float32) / 64)
-    angles = positions.astype(jnp.float32)[:, None] * spacing[None, :]
-    cosine, sine = jnp.cos(angles), jnp.sin(angles)
-    lru_state, conv_state, kv_cache = prefill(
-        transport_block(w_x),
+    lru_state, conv_state, cache_columns = prefill(
+        lengths,
         tokens[0],
         attn_in[0],
         w_kv,
         w_a,
         w_i,
-        tokens[0, local_len - 4 :],
-        jnp.broadcast_to(lengths[0], (8, 128)),
+        w_x,
         norm_gain[None],
         attn_gain[None],
+        lru_decay[None],
         conv_w,
-        (-8.0 * jax.nn.softplus(-lru_decay))[None],
-        jnp.concatenate([cosine, cosine], axis=1),
-        jnp.concatenate([-sine, sine], axis=1),
     )
-    return (lru_state, conv_state[None], kv_cache[None])
+    return (lru_state, conv_state[None], cache_columns.T[None])
 
 
 def solution(mesh):

time: 110 us -> 91.6 us (0.83)
  the two profiles are of different devices: /device:TPU:33 before, /device:TPU:101 now
where the time goes in v1:
time: 91.6 us; the launch traced here: 91.3 us
  Pallas kernels  86.1 us (94%)
  local copies, waits for them, and re-layouts  3.93 us (4%)
  between operations  1.29 us (1%)
    pallas_call x1, Pallas kernels, prefill(): pl.pallas_call(prefill_kernel, out_shape=(jax.ShapeDtypeStruct((8, 8, 384...  84.2 us
    pallas_call x1, Pallas kernels, prefill(): pl.pallas_call(finish_kernel, out_shape=(jax.ShapeDtypeStruct((1, feature...  1.95 us

profile of v1, /device:TPU:101, one launch (start us, length us, event | category | flops | bytes accessed | tf_op | source)
XLA Modules:
  0.0 91.3 jit_solution(3350522655835186029)
XLA Ops:
  1.3 1.3 %broadcast_in_dim.15.gain_ref = f32[1,2560]{1,0:T(1,128)} reshape(f32[2560]{0:T(1024)} %param.17) | data formatting | bytes 20480 | tf_op jit(solution)/shard_map/broadcast_in_dim | solution.py:628
  2.6 1.3 %broadcast_in_dim.16.attn_gain_ref = f32[1,2560]{1,0:T(1,128)} reshape(f32[2560]{0:T(1024)} %param.18) | data formatting | bytes 20480 | tf_op jit(solution)/shard_map/broadcast_in_dim | solution.py:629
  3.9 1.3 %broadcast_in_dim.17.decay_ref = f32[1,2560]{1,0:T(1,128)} reshape(f32[2560]{0:T(1024)} %param.23) | data formatting | bytes 20480 | tf_op jit(solution)/shard_map/broadcast_in_dim | solution.py:630
  5.2 84.2 %shard_map.157 = (f32[8,8,384]{2,1,0:T(8,128)}, bf16[8,256,128]{2,1,0:T(8,128)(2,1)}) custom-call(s32[1]{0:T(128)S(6)} %copy.17.length_in, bf16[512,2560]{1,0:T(8,128)(2,1)} %bitcast.6, bf16[512,2560]{1,0:T(8,128)(2,1)} %bitcast.7, bf16[2560,512]{1,0:T(8,128)(2,1)} %wkv_hbm.1, bf16[10,256,256]{2,1,0:T(8,128)(2,1)} %wa_hbm.1, bf16[10,256,256]{2,1,0:T(8,128)(2,1)} %wi_hbm.1, ...), custom_call_target="tpu_custom_call" | custom-call | tf_op jit(solution)/shard_map/pallas_call | solution.py:561
  89.4 1.9 %shard_map.158 = (f32[1,320]{1,0:T(1,128)}, bf16[3,320]{1,0:T(4,128)(2,1)}, bf16[64,2048]{1,0:T(8,128)(2,1)}) custom-call(f32[8,8,384]{2,1,0:T(8,128)} %get-tuple-element.8.arrived, bf16[8,256,128]{2,1,0:T(8,128)(2,1)} %get-tuple-element.9.cached), custom_call_target="tpu_custom_call" | custom-call | tf_op jit(solution)/shard_map/pallas_call | solution.py:605

commit v2 on v1

--- a/solution.py
+++ b/solution.py
@@ -17,7 +17,24 @@
 MESH_ID = pl.DeviceIdType.MESH
 
 RING = {"x": 4, "y": 4, "z": 8}
-PLANS = ((0, 5, "xyz"), (5, 4, "zxy"), (9, 4, "zyx"))
+PLANS = (
+    (0, 2, "zyx", None),
+    (2, 2, "zxy", None),
+    (4, 2, "zyx", None),
+    (6, 2, "zxy", None),
+    (8, 2, "xzy", (5, 0)),
+    (10, 3, "yxz", None),
+)
+TASKS = (
+    (0.0, 2.4),
+    (9.8, 2.0),
+    (12.1, 1.0),
+    (14.4, 2.0),
+    (16.7, 2.0),
+    (19.0, 2.6),
+    (21.3, 2.6),
+    (23.5, 1.0),
+)
 HEADS = 5
 COLS = HEADS * HD
 WIDE = 13 * 128
@@ -26,70 +43,82 @@
 HALO = 16
 
 
-def phase_copies(share, phase):
-    size = RING[PLANS[share][2][phase]]
+def phase_copies(plans, share, phase):
+    size = RING[plans[share][2][phase]]
     copies = []
     for step in range(size // 2):
-        for way in (1, -1):
-            for half in (0, 1):
+        for half in (0, 1):
+            for way in (1, -1):
                 if step < size // 2 - 1 or half == (way < 0):
                     copies.append((share, phase, way, step, half))
     return copies
 
 
-def gather_schedule():
-    copies = [c for s in range(3) for p in range(3) for c in phase_copies(s, p)]
+def gather_schedule(plans, task_times):
+    count = len(plans)
+    waiting, copies = {}, []
+    for share in range(count):
+        for phase in range(3):
+            for c in phase_copies(plans, share, phase):
+                _, _, way, step, half = c
+                if step:
+                    waiting[c] = {(share, phase, way, step - 1, half)}
+                elif phase:
+                    waiting[c] = set(phase_copies(plans, share, phase - 1))
+                else:
+                    gate = plans[share][3]
+                    waiting[c] = set(phase_copies(plans, *gate)) if gate else set()
+                copies.append(c)
+    readers = {}
+    for c in copies:
+        for need in waiting[c]:
+            readers.setdefault(need, []).append(c)
     index = {c: k for k, c in enumerate(copies)}
-    waiting = {}
-    for c in copies:
-        share, phase, way, step, half = c
-        if step:
-            waiting[c] = {(share, phase, way, step - 1, half)}
-        else:
-            waiting[c] = set(phase_copies(share, phase - 1)) if phase else set()
+    missing = [sum(c[0] == s for c in copies) for s in range(count)]
     free, arrivals, order = {}, [], []
-
-    def send(c, now):
+    now, stage = 0.0, 0
+    tasks = list(enumerate(task_times))
+
+    def send(c):
         share, phase, way, _, _ = c
-        volume = PLANS[share][1]
-        for dim in PLANS[share][2][:phase]:
+        volume = plans[share][1]
+        for dim in plans[share][2][:phase]:
             volume *= RING[dim]
-        link = (PLANS[share][2][phase], way)
+        link = (plans[share][2][phase], way)
         free[link] = max(now, free.get(link, 0.0)) + volume * 2048 / 46.6e3
         heapq.heappush(arrivals, (free[link] + 1.8, index[c]))
-        order.append(("send", index[c], now))
-
-    for c in copies:
-        if not waiting[c]:
-            send(c, 0.0)
-    while arrivals:
-        now, k = heapq.heappop(arrivals)
-        order.append(("recv", k, now))
+        order.append(("send", index[c]))
+
+    for half in (0, 1):
         for c in copies:
-            if copies[k] in waiting[c]:
-                waiting[c].discard(copies[k])
-                if not waiting[c]:
-                    send(c, now)
+            if not waiting[c] and c[4] == half:
+                send(c)
+        order.append(("half", half))
+    while arrivals or stage < count - 1:
+        while arrivals and arrivals[0][0] <= now:
+            c = copies[heapq.heappop(arrivals)[1]]
+            order.append(("recv", index[c]))
+            missing[c[0]] -= 1
+            for d in readers.get(c, ()):
+                waiting[d].discard(c)
+                if not waiting[d]:
+                    send(d)
+        if tasks and tasks[0][1][0] <= now:
+            number, (_, length) = tasks.pop(0)
+            order.append(("task", number))
+            now += length
+        elif stage < count - 1 and not missing[stage] and not missing[-1] and not tasks:
+            order.append(("stage", stage))
+            now += 3.2 if stage else 2.6
+            stage += 1
+        else:
+            pend = [arrivals[0][0]] if arrivals else []
+            if tasks:
+                pend.append(tasks[0][1][0])
+            now = max(now, min(pend))
     return copies, order
 
-
-COPIES, ORDER = gather_schedule()
-
-
-def column_orders():
-    order = np.zeros((640, 640), np.float32)
-    for q in range(64):
-        x, core, y, z_hi = q // 16, q // 8 % 2, q // 2 % 4, q % 2
-        spot = x * 8 + y * 2 + core
-        for i in range(10):
-            if i < 8:
-                order[10 * q + i, z_hi * 256 + spot * 8 + i] = 1
-            else:
-                order[10 * q + i, 512 + (i - 8) * 64 + z_hi * 32 + spot] = 1
-    sort = np.zeros((256, 256), np.float32)
-    for row in range(256):
-        sort[row, row % 32 * 8 + row // 32] = 1
-    return jnp.asarray(order, jnp.bfloat16), jnp.asarray(sort, jnp.bfloat16)
+COPIES, ORDER = gather_schedule(PLANS, TASKS)
 
 
 def f32_dot(a, b):
@@ -118,8 +147,6 @@
     attn_gain_ref,
     decay_ref,
     conv_ref,
-    order_ref,
-    sort_ref,
     trig_ref,
     arrived,
     cached,
@@ -133,6 +160,8 @@
     wkv,
     gates,
     halo,
+    order_ref,
+    sort_ref,
     tail_rows,
     lengths_ref,
     block,
@@ -223,14 +252,30 @@
         block[side, :, COLS:] = rest_tiles[side].astype(jnp.bfloat16)
     wide[mine] = block[pl.ds(core, 1)]
     lengths_ref[0] = jnp.full((8, 128), length_in[0], jnp.int32)
-    spread = jnp.exp(-decay_ref[...])
+    spread = jnp.exp(-decay_ref[...][None])
     series = 1.0 / 5.0 - spread * (1.0 / 6.0)
     for c in (1.0 / 4.0, 1.0 / 3.0, 0.5, 1.0):
         series = c - spread * series
     fall[...] = (8.0 * spread) * series
 
+    feature = lax.broadcasted_iota(jnp.int32, (640, 1), 0)
+    unit = (feature * 6554) >> 16
+    i = feature - 10 * unit
+    spot = (unit >> 4) * 8 + ((unit >> 1) & 3) * 2 + ((unit >> 3) & 1)
+    target = jnp.where(
+        i < 8,
+        (unit & 1) * 256 + spot * 8 + i,
+        512 + (i - 8) * 64 + (unit & 1) * 32 + spot,
+    )
+    lanes = lax.broadcasted_iota(jnp.int32, (640, 640), 1)
+    order_ref[...] = (lanes == target).astype(jnp.float32).astype(jnp.bfloat16)
+    row = lax.broadcasted_iota(jnp.int32, (256, 1), 0)
+    lanes = lax.broadcasted_iota(jnp.int32, (256, 256), 1)
+    source = (row & 31) * 8 + (row >> 5)
+    sort_ref[...] = (lanes == source).astype(jnp.float32).astype(jnp.bfloat16)
+
     def place_rows(slot, start, raw):
-        normed = normed_rows(raw, gain_ref[...])
+        normed = normed_rows(raw, gain_ref[...][None])
         at = pl.ds(slot * span + start, raw.shape[0])
         for g in range(4):
             moved = f32_dot(normed[:, 640 * g : 640 * (g + 1)], order_ref[...])
@@ -261,7 +306,7 @@
         tops = []
         lane = lax.broadcasted_iota(jnp.int32, (128, 128), 1)
         for start in (128 * k, 256 + 128 * k):
-            normed = normed_rows(attn[start : start + 128, :], attn_gain_ref[...])
+            normed = normed_rows(attn[start : start + 128, :], attn_gain_ref[...][None])
             kv = f32_dot(normed, wkv[...])
             cosine, sine = rotation(start)
             turned = kv[:, :128] * cosine + pltpu.roll(kv[:, :128], 64, 1) * sine
@@ -291,7 +336,7 @@
 
     def gather_copy(k):
         share, phase, way, step, half = COPIES[k]
-        first, count, order = PLANS[share]
+        first, count, order, _ = PLANS[share]
         dim = order[phase]
         spans = {d: pl.ds(0, RING[d]) for d in order[:phase]}
         spot = lax.rem(me[dim] - way * step + RING[dim], RING[dim])
@@ -302,7 +347,7 @@
             spans["y"] = pl.ds(4 * half, 4)
         else:
             y_at = spot if dim == "y" else me["y"]
-            spans["y"] = pl.ds(2 * y_at + half, 1)
+            spans["y"] = pl.ds(2 * y_at + lax.rem(core + half, 2), 1)
         piece = wide.at[
             spans["z"], spans["x"], spans["y"], pl.ds(0, 8), pl.ds(first * 128, count * 128)
         ]
@@ -333,28 +378,16 @@
         passed.wait()
         edge_rows(1)
 
-    tasks = [
-        (0.0, start_own),
-        (10.0, lambda: body_rows(0, 1)),
-        (14.0, pass_halo),
-        (16.0, start_other),
-        (19.0, lambda: body_rows(1, 1)),
-        (22.0, start_cache),
-        (25.0, lambda: cache_rows(1)),
-        (28.0, end_halo),
-    ]
-    given.wait()
-    started = {}
-    for what, k, when in ORDER:
-        if what == "send":
-            started[k] = gather_copy(k)
-            started[k].start()
-        else:
-            while tasks and tasks[0][0] <= when:
-                tasks.pop(0)[1]()
-            started[k].wait_recv()
-    for _, task in tasks:
-        task()
+    tasks = (
+        start_own,
+        lambda: body_rows(0, 1),
+        pass_halo,
+        start_other,
+        lambda: body_rows(1, 1),
+        start_cache,
+        lambda: cache_rows(1),
+        end_halo,
+    )
 
     def kv_copy(turn):
         spot = lax.rem(place + turn, 8)
@@ -368,20 +401,14 @@
         )
 
     kv_copies = [kv_copy(turn) for turn in range(1, 8)]
-    for copy in kv_copies:
-        copy.start()
     local = pltpu.make_async_copy(packed.at[place], cached.at[place], local_sem.at[5])
-    local.start()
-    fetches[3].wait()
-    fetches[4].wait()
-    length_copy.wait()
-
-    for z in range(8):
-        rest = wide[z, :, :, :, COLS:].reshape(256, WIDE - COLS)
-        sorted_rows = f32_dot(sort_ref[...], rest).astype(jnp.bfloat16)
-        for r in range(2):
-            for j in range(10):
-                unit = r * 10 + j
+
+    def sort_rest():
+        for z in range(8):
+            rest = wide[z, :, :, :, COLS:].reshape(256, WIDE - COLS)
+            sorted_rows = f32_dot(sort_ref[...], rest).astype(jnp.bfloat16)
+            for unit in range(20):
+                r, j = unit // 10, unit % 10
                 row = z % 4 * 128 + r * 64 + z // 4 * 32
                 left[row : row + 32, 128 * j : 128 * (j + 1)] = sorted_rows[
                     32 * (unit % 8) : 32 * (unit % 8) + 32,
@@ -392,10 +419,9 @@
         lax.broadcasted_iota(jnp.int32, (256, 256), 1)
         > lax.broadcasted_iota(jnp.int32, (256, 256), 0)
     ).astype(jnp.bfloat16)
-    lengths = (length, lengths_ref[1, 0:1, 0:1])
 
     def of_head(head):
-        return pl.ds(pl.multiple_of(head * HD, HD), HD)
+        return pl.ds(head * HD, HD)
 
     def project(head, proj):
         weight = wide[:, :, :, :, of_head(head)].reshape(MAIN, HD)
@@ -404,6 +430,7 @@
         proj[...] = total.astype(jnp.bfloat16).astype(jnp.float32)
 
     def fold(head, proj):
+        lengths = (length, lengths_ref[1, 0:1, 0:1])
         columns = of_head(head)
         channels = pl.ds(pl.multiple_of((HEADS * core + head) * HD, HD), HD)
         taps = conv_ref[:, channels]
@@ -449,17 +476,38 @@
             sums[slot, 1:2, columns] = state
             sums[slot, 2:5, columns] = picked[0:3]
 
-    def head_pair(k, carry):
-        project(2 * k + 1, proj_odd)
-        fold(2 * k, proj_even)
-        project(2 * k + 2, proj_even)
-        fold(2 * k + 1, proj_odd)
-        return carry
+    projs = (proj_even, proj_odd)
+
+    def head_stage(head):
+        if head == 0:
+            fetches[3].wait()
+            fetches[4].wait()
+            length_copy.wait()
+            sort_rest()
+        project(head, projs[head % 2])
+        if head:
+            fold(head - 1, projs[(head - 1) % 2])
 
     sums[...] = jnp.zeros_like(sums)
-    project(0, proj_even)
-    lax.fori_loop(0, HEADS // 2, head_pair, 0)
-    fold(HEADS - 1, proj_even)
+    started = {}
+    last_send = max(n for n, (what, _) in enumerate(ORDER) if what == "send")
+    for n, (what, k) in enumerate(ORDER):
+        if what == "send":
+            started[k] = gather_copy(k)
+            started[k].start()
+        elif what == "recv":
+            started[k].wait_recv()
+        elif what == "task":
+            tasks[k]()
+        elif what == "stage":
+            head_stage(k)
+        elif k == 0:
+            given.wait()
+        if n == last_send:
+            local.start()
+            for copy in kv_copies:
+                copy.start()
+    fold(HEADS - 1, projs[(HEADS - 1) % 2])
 
     for slot in range(2):
         for k in range(4):
@@ -552,7 +600,6 @@
 
 
 def prefill(length, tokens, attn_in, w_kv, w_a, w_i, shard, gain, attn_gain, decay, conv_w):
-    order, sort = column_orders()
     local_len, feature_dim = tokens.shape
     vmem = pl.BlockSpec(memory_space=pltpu.VMEM)
     hbm = pl.BlockSpec(memory_space=pl.ANY)
@@ -564,7 +611,7 @@
             jax.ShapeDtypeStruct((8, 8, 384), jnp.float32),
             jax.ShapeDtypeStruct((8, local_len // 2, 128), jnp.bfloat16),
         ),
-        in_specs=[pl.BlockSpec(memory_space=pltpu.SMEM)] + [hbm] * 5 + [vmem] * 8,
+        in_specs=[pl.BlockSpec(memory_space=pltpu.SMEM)] + [hbm] * 5 + [vmem] * 6,
         out_specs=(hbm, hbm),
         scratch_shapes=[
             pltpu.VMEM((8, 4, 8, 8, WIDE), jnp.bfloat16),
@@ -577,6 +624,8 @@
             pltpu.VMEM(w_kv.shape, jnp.bfloat16),
             pltpu.VMEM((2, HEADS, HD, HD), jnp.bfloat16),
             pltpu.VMEM((2, 4, feature_dim), jnp.bfloat16),
+            pltpu.VMEM((640, 640), jnp.bfloat16),
+            pltpu.VMEM((256, 256), jnp.bfloat16),
             pltpu.VMEM((4, feature_dim), jnp.bfloat16),
             pltpu.VMEM((2, 8, 128), jnp.int32),
             pltpu.VMEM((2, 8, WIDE), jnp.bfloat16),
@@ -600,7 +649,7 @@
         ),
     )(
         length, tokens, attn_in, w_kv, w_a, w_i, shard, gain, attn_gain, decay, conv_w,
-        order, sort, rotation_tables(),
+        rotation_tables(),
     )
     return pl.pallas_call(
         finish_kernel,
@@ -625,9 +674,9 @@
         w_a,
         w_i,
         w_x,
-        norm_gain[None],
-        attn_gain[None],
-        lru_decay[None],
+        norm_gain,
+        attn_gain,
+        lru_decay,
         conv_w,
     )
     return (lru_state, conv_state[None], cache_columns.T[None])

time: 91.6 us -> 83.8 us (0.915)
  the two profiles are of different devices: /device:TPU:101 before, /device:TPU:1 now
where the time goes in v2:
time: 83.8 us; the launch traced here: 83.7 us
  Pallas kernels  82.4 us (98%)
  between operations  1.29 us (2%)
    pallas_call x1, Pallas kernels, prefill(): pl.pallas_call(prefill_kernel, out_shape=(jax.ShapeDtypeStruct((8, 8, 384...  80.5 us
    pallas_call x1, Pallas kernels, prefill(): pl.pallas_call(finish_kernel, out_shape=(jax.ShapeDtypeStruct((1, feature...  1.95 us

profile of v2, /device:TPU:1, one launch (start us, length us, event | category | flops | bytes accessed | tf_op | source)
XLA Modules:
  0.0 83.7 jit_solution(11064592700113807803)
XLA Ops:
  1.3 80.5 %shard_map.139 = (f32[8,8,384]{2,1,0:T(8,128)}, bf16[8,256,128]{2,1,0:T(8,128)(2,1)}) custom-call(s32[1]{0:T(128)S(6)} %copy.15.length_in, bf16[512,2560]{1,0:T(8,128)(2,1)} %bitcast.6, bf16[512,2560]{1,0:T(8,128)(2,1)} %bitcast.7, bf16[2560,512]{1,0:T(8,128)(2,1)} %wkv_hbm.1, bf16[10,256,256]{2,1,0:T(8,128)(2,1)} %wa_hbm.1, bf16[10,256,256]{2,1,0:T(8,128)(2,1)} %wi_hbm.1, ...), custom_call_target="tpu_custom_call" | custom-call | tf_op jit(solution)/shard_map/pallas_call | solution.py:608
  81.8 1.9 %shard_map.140 = (f32[1,320]{1,0:T(1,128)}, bf16[3,320]{1,0:T(4,128)(2,1)}, bf16[64,2048]{1,0:T(8,128)(2,1)}) custom-call(f32[8,8,384]{2,1,0:T(8,128)} %get-tuple-element.8.arrived, bf16[8,256,128]{2,1,0:T(8,128)(2,1)} %get-tuple-element.9.cached), custom_call_target="tpu_custom_call" | custom-call | tf_op jit(solution)/shard_map/pallas_call | solution.py:654

commit v3 on v2

--- a/solution.py
+++ b/solution.py
@@ -18,22 +18,22 @@
 
 RING = {"x": 4, "y": 4, "z": 8}
 PLANS = (
-    (0, 2, "zyx", None),
-    (2, 2, "zxy", None),
-    (4, 2, "zyx", None),
+    (0, 2, "zxy", None),
+    (2, 2, "zyx", None),
+    (4, 2, "yzx", None),
     (6, 2, "zxy", None),
-    (8, 2, "xzy", (5, 0)),
-    (10, 3, "yxz", None),
+    (8, 2, "zxy", (1, 0)),
+    (10, 3, "xyz", None),
 )
 TASKS = (
-    (0.0, 2.4),
-    (9.8, 2.0),
-    (12.1, 1.0),
-    (14.4, 2.0),
-    (16.7, 2.0),
-    (19.0, 2.6),
-    (21.3, 2.6),
-    (23.5, 1.0),
+    (0.0, 2.8),
+    (11.0, 1.6),
+    (13.7, 0.7),
+    (16.4, 1.6),
+    (19.0, 1.6),
+    (21.7, 2.2),
+    (24.4, 2.0),
+    (27.1, 0.7),
 )
 HEADS = 5
 COLS = HEADS * HD
@@ -61,7 +61,7 @@
         for phase in range(3):
             for c in phase_copies(plans, share, phase):
                 _, _, way, step, half = c
-                if step:
+                if phase and step:
                     waiting[c] = {(share, phase, way, step - 1, half)}
                 elif phase:
                     waiting[c] = set(phase_copies(plans, share, phase - 1))
@@ -80,13 +80,14 @@
     tasks = list(enumerate(task_times))
 
     def send(c):
-        share, phase, way, _, _ = c
-        volume = plans[share][1]
+        share, phase, way, step, _ = c
+        hops = 1 if phase else step + 1
+        volume = plans[share][1] * hops
         for dim in plans[share][2][:phase]:
             volume *= RING[dim]
         link = (plans[share][2][phase], way)
         free[link] = max(now, free.get(link, 0.0)) + volume * 2048 / 46.6e3
-        heapq.heappush(arrivals, (free[link] + 1.8, index[c]))
+        heapq.heappush(arrivals, (free[link] + 1.6 + 0.7 * hops, index[c]))
         order.append(("send", index[c]))
 
     for half in (0, 1):
@@ -109,7 +110,7 @@
             now += length
         elif stage < count - 1 and not missing[stage] and not missing[-1] and not tasks:
             order.append(("stage", stage))
-            now += 3.2 if stage else 2.6
+            now += 3.0 if stage else 2.6
             stage += 1
         else:
             pend = [arrivals[0][0]] if arrivals else []
@@ -117,7 +118,6 @@
                 pend.append(tasks[0][1][0])
             now = max(now, min(pend))
     return copies, order
-
 COPIES, ORDER = gather_schedule(PLANS, TASKS)
 
 
@@ -203,7 +203,8 @@
     after = beside(lax.rem(place + 1, 8), core)
 
     barrier = pltpu.get_barrier_semaphore()
-    friends = [toward(d, w) for d in "xz" for w in (1, -1)]
+    friends = [toward("x", away) for away in (1, 2, 3)]
+    friends += [toward("z", away) for away in (1, 2, 3, -1, -2, -3)]
     for turn in range(8):
         for flip in range(2):
             if turn or flip:
@@ -252,28 +253,6 @@
         block[side, :, COLS:] = rest_tiles[side].astype(jnp.bfloat16)
     wide[mine] = block[pl.ds(core, 1)]
     lengths_ref[0] = jnp.full((8, 128), length_in[0], jnp.int32)
-    spread = jnp.exp(-decay_ref[...][None])
-    series = 1.0 / 5.0 - spread * (1.0 / 6.0)
-    for c in (1.0 / 4.0, 1.0 / 3.0, 0.5, 1.0):
-        series = c - spread * series
-    fall[...] = (8.0 * spread) * series
-
-    feature = lax.broadcasted_iota(jnp.int32, (640, 1), 0)
-    unit = (feature * 6554) >> 16
-    i = feature - 10 * unit
-    spot = (unit >> 4) * 8 + ((unit >> 1) & 3) * 2 + ((unit >> 3) & 1)
-    target = jnp.where(
-        i < 8,
-        (unit & 1) * 256 + spot * 8 + i,
-        512 + (i - 8) * 64 + (unit & 1) * 32 + spot,
-    )
-    lanes = lax.broadcasted_iota(jnp.int32, (640, 640), 1)
-    order_ref[...] = (lanes == target).astype(jnp.float32).astype(jnp.bfloat16)
-    row = lax.broadcasted_iota(jnp.int32, (256, 1), 0)
-    lanes = lax.broadcasted_iota(jnp.int32, (256, 256), 1)
-    source = (row & 31) * 8 + (row >> 5)
-    sort_ref[...] = (lanes == source).astype(jnp.float32).astype(jnp.bfloat16)
-
     def place_rows(slot, start, raw):
         normed = normed_rows(raw, gain_ref[...][None])
         at = pl.ds(slot * span + start, raw.shape[0])
@@ -339,7 +318,9 @@
         first, count, order, _ = PLANS[share]
         dim = order[phase]
         spans = {d: pl.ds(0, RING[d]) for d in order[:phase]}
-        spot = lax.rem(me[dim] - way * step + RING[dim], RING[dim])
+        away = way if phase else way * (step + 1)
+        back = way * step if phase else 0
+        spot = lax.rem(me[dim] - back + RING[dim], RING[dim])
         spans[dim] = pl.ds(spot, 1)
         for d in order[phase + 1 :]:
             spans[d] = pl.ds(me[d], 1)
@@ -351,9 +332,30 @@
         piece = wide.at[
             spans["z"], spans["x"], spans["y"], pl.ds(0, 8), pl.ds(first * 128, count * 128)
         ]
-        return remote(piece, piece, (send_sem, recv_sem), k, toward(dim, way))
+        return remote(piece, piece, (send_sem, recv_sem), k, toward(dim, away))
 
     def start_own():
+        spread = jnp.exp(-decay_ref[...][None])
+        series = 1.0 / 5.0 - spread * (1.0 / 6.0)
+        for c in (1.0 / 4.0, 1.0 / 3.0, 0.5, 1.0):
+            series = c - spread * series
+        fall[...] = (8.0 * spread) * series
+
+        feature = lax.broadcasted_iota(jnp.int32, (640, 1), 0)
+        unit = (feature * 6554) >> 16
+        i = feature - 10 * unit
+        spot = (unit >> 4) * 8 + ((unit >> 1) & 3) * 2 + ((unit >> 3) & 1)
+        target = jnp.where(
+            i < 8,
+            (unit & 1) * 256 + spot * 8 + i,
+            512 + (i - 8) * 64 + (unit & 1) * 32 + spot,
+        )
+        lanes = lax.broadcasted_iota(jnp.int32, (640, 640), 1)
+        order_ref[...] = (lanes == target).astype(jnp.float32).astype(jnp.bfloat16)
+        row = lax.broadcasted_iota(jnp.int32, (256, 1), 0)
+        lanes = lax.broadcasted_iota(jnp.int32, (256, 256), 1)
+        source = (row & 31) * 8 + (row >> 5)
+        sort_ref[...] = (lanes == source).astype(jnp.float32).astype(jnp.bfloat16)
         fetches[0].wait()
         last = rows[0, local_len - 8 :, :].astype(jnp.float32)
         tail_rows[...] = last[4:].astype(jnp.bfloat16)

time: 83.8 us -> 79.6 us (0.950)
  Pallas kernels: 82.4 us -> 78.1 us
    pallas_call x1, Pallas kernels: 80.5 us -> 76.2 us  [prefill(): pl.pallas_call(prefill_kernel, out_shape=(jax.ShapeDtypeStruct((8, 8, 384...]
where the time goes in v3:
time: 79.6 us; the launch traced here: 79.4 us
  Pallas kernels  78.1 us (98%)
  between operations  1.29 us (2%)
    pallas_call x1, Pallas kernels, prefill(): pl.pallas_call(prefill_kernel, out_shape=(jax.ShapeDtypeStruct((8, 8, 384...  76.2 us
    pallas_call x1, Pallas kernels, prefill(): pl.pallas_call(finish_kernel, out_shape=(jax.ShapeDtypeStruct((1, feature...  1.95 us

profile of v3, /device:TPU:1, one launch (start us, length us, event | category | flops | bytes accessed | tf_op | source)
XLA Modules:
  0.0 79.4 jit_solution(13313956298803444509)
XLA Ops:
  1.3 76.2 %shard_map.139 = (f32[8,8,384]{2,1,0:T(8,128)}, bf16[8,256,128]{2,1,0:T(8,128)(2,1)}) custom-call(s32[1]{0:T(128)S(6)} %copy.15.length_in, bf16[512,2560]{1,0:T(8,128)(2,1)} %bitcast.6, bf16[512,2560]{1,0:T(8,128)(2,1)} %bitcast.7, bf16[2560,512]{1,0:T(8,128)(2,1)} %wkv_hbm.1, bf16[10,256,256]{2,1,0:T(8,128)(2,1)} %wa_hbm.1, bf16[10,256,256]{2,1,0:T(8,128)(2,1)} %wi_hbm.1, ...), custom_call_target="tpu_custom_call" | custom-call | tf_op jit(solution)/shard_map/pallas_call | solution.py:610
  77.5 1.9 %shard_map.140 = (f32[1,320]{1,0:T(1,128)}, bf16[3,320]{1,0:T(4,128)(2,1)}, bf16[64,2048]{1,0:T(8,128)(2,1)}) custom-call(f32[8,8,384]{2,1,0:T(8,128)} %get-tuple-element.8.arrived, bf16[8,256,128]{2,1,0:T(8,128)(2,1)} %get-tuple-element.9.cached), custom_call_target="tpu_custom_call" | custom-call | tf_op jit(solution)/shard_map/pallas_call | solution.py:656
